TPU v7x, 32 devices: a whole 2x2x4 slice. The times are simulated.
32 devices in a mesh: blk: 4 (over y, x), grp: 8 (over z, core).
Axes of the slice: x: 2, y: 2, z: 4, core: 2. Of those that a mesh axis runs over, the one named last changes fastest.
Arguments:
- b3c: bfloat16 [384, 3, 32, 4096], P('blk', None, None, 'grp'), may hold values from -6 to 6
- green_occ: bfloat16 [384, 384], P('blk', 'grp'), may hold values from -0.3125 to 0.3125
- green_virt: bfloat16 [384, 384], P(None, 'grp'), may hold values from -0.625 to 0.625
- occ_mask: int32 [12, 12], replicated, may hold values from 0 to 1, as said below
- a_tiles: bfloat16 [128, 32, 1024], P(('blk', 'grp')), may hold values from -0.046875 to 0.046875
- tile_codes: int32 [128], P(('blk', 'grp')), may hold values from -1 to 143, as said below
Outputs:
- chi: float32 [512, 4096], P('blk', 'grp')
Inputs may be any that keep to these rules, and one draw needn't show every extreme that they name: `occ_mask`: the diagonal is 1. `tile_codes`: each device's 4 slots hold its live tiles first and -1 after them; some device has all 4 slots live; codes may repeat, and repeated tiles add.
All inputs are finite; a program needn't handle non-finite values.
Results may differ from a plain program's by a relative error of at most 0.0041.
Values may be sent and summed in bfloat16 or wider, within the bound.
No kernel may reach another device: no remote copies, remote signals or barrier semaphores. Data moves between devices by JAX's collectives and lax.ppermute only.
A program may use at most 192 MiB of HBM per device.

v0:
```python
import jax
import jax.numpy as jnp
from jax import lax
from jax.sharding import PartitionSpec as P

BS = 32
PB = 32
KB = 3
BAND = 3
PBD = 4


def local(b3c, green_occ, green_virt, occ_mask, a_tiles, tile_codes):
    group = lax.axis_index("blk")
    occ_all, virt_all = (
        lax.all_gather(green_occ, "grp", axis=1, tiled=True),
        lax.all_gather(green_virt, "grp", axis=1, tiled=True),
    )
    basis_total = virt_all.shape[1]
    block_total = basis_total // BS
    window = (KB + BAND - 1) * BS
    pair_count = KB * BAND
    query_local = b3c.shape[3]
    mask_rows = lax.dynamic_slice_in_dim(occ_mask, group * KB, KB, 0)
    mask_full = jnp.repeat(jnp.repeat(mask_rows, BS, axis=0), BS, axis=1).astype(jnp.bfloat16)
    occ_group = occ_all * mask_full
    rows = (group * KB * BS + jnp.arange(window, dtype=jnp.int32)) % basis_total
    virt_window = jnp.take(virt_all, rows, axis=0).reshape(window, block_total, BS)
    accumulate_piece = lax.all_gather(b3c, "blk", axis=0, tiled=True)
    count = accumulate_piece.shape[0]
    blocks_in = count // BS
    lam_index = jnp.arange(count, dtype=jnp.int32) % basis_total
    occ_cols = jnp.take(occ_group, lam_index, axis=1)
    lam_blocks = jnp.arange(blocks_in, dtype=jnp.int32) % block_total
    partner = (lam_blocks[:, None] + jnp.arange(BAND, dtype=jnp.int32)[None, :]) % block_total
    virt_sel = jnp.take(virt_window, partner, axis=1)
    tensor = accumulate_piece.reshape(blocks_in, BS, BAND, BS, query_local)
    inner = jnp.einsum("wlds,ladsq->lawq", virt_sel, tensor, preferred_element_type=jnp.float32)
    inner = inner.astype(jnp.bfloat16).reshape(count, window * query_local)
    paired = jnp.dot(occ_cols, inner, preferred_element_type=jnp.float32)
    paired = paired.reshape(KB * BS, window, query_local).astype(jnp.bfloat16)
    pieces = []
    for block in range(KB):
        for offset in range(BAND):
            piece = paired[
                block * BS : (block + 1) * BS, (block + offset) * BS : (block + offset + 1) * BS
            ]
            pieces.append(piece.reshape(BS * BS, query_local))
    pairs = jnp.stack(pieces)
    aux_blocks = lax.axis_size("blk") * PBD
    tiles = lax.all_gather(a_tiles, "grp", axis=0, tiled=True)
    codes = lax.all_gather(tile_codes, "grp", axis=0, tiled=True)
    count = tiles.shape[0]
    valid = codes >= 0
    pair = jnp.where(valid, codes % pair_count, 0).astype(jnp.int32)
    pblock = jnp.where(valid, codes // pair_count, -1).astype(jnp.int32)
    chosen = jnp.take(pairs, pair, axis=0)
    contrib = jnp.einsum("tik,tkq->tiq", tiles, chosen, preferred_element_type=jnp.float32)
    selector = (jnp.arange(aux_blocks, dtype=jnp.int32)[:, None] == pblock[None, :]).astype(
        jnp.float32
    )
    partial_chi = jnp.dot(
        selector, contrib.reshape(count, PB * query_local), precision=lax.Precision.HIGHEST
    )
    partial_chi = partial_chi.reshape(aux_blocks * PB, query_local)
    return lax.psum_scatter(partial_chi, "blk", scatter_dimension=0, tiled=True)


def solution(mesh):
    in_specs = (
        P("blk", None, None, "grp"),
        P("blk", "grp"),
        P(None, "grp"),
        P(),
        P(("blk", "grp"), None, None),
        P(("blk", "grp")),
    )
    out_specs = P("blk", "grp")
    return jax.shard_map(local, mesh=mesh, in_specs=in_specs, out_specs=out_specs, check_vma=False)
```

profile of v0, /device:TPU:0, one launch (start us, length us, event | category | flops | bytes accessed | tf_op | source)
XLA Modules:
  0.0 637.7 jit_solution(16914202088193835434)
XLA Ops:
  6.6 0.7 all-gather.3.cloned.1.call-update
  7.3 0.7 all-gather.5.cloned.1.call-update
  8.2 0.6 dynamic-slice
  9.4 0.2 dynamic-update-slice
  9.7 10.6 %all-reduce = s32[32]{0:T(128)S(1)} all-reduce(s32[32]{0:T(128)S(1)} %dynamic-update-slice), channel_id=1, replica_groups=mesh['blk'=4,'grp'=8] {'grp'}, use_global_device_ids=true, to_apply=%add | all-reduce | flops 32 | bytes 256
  20.3 0.5 compare_and_fusion.2
  20.9 0.5 compare_select_fusion.6
  21.4 0.7 dynamic-slice_convert_fusion
  22.1 0.1 copy.26
  22.3 0.1 convert_element_type.22
  22.4 13.9 %all_gather.16 = bf16[96,384]{0,1:T(8,128)(2,1)S(1)} all-gather(bf16[96,48]{0,1:T(8,128)(2,1)S(1)} %copy-done.1), channel_id=1, replica_groups=mesh['blk'=4,'grp'=8] {'grp'}, dimensions={1}, use_global_device_ids=true | all-gather | bytes 82944 | tf_op jit(solution)/shard_map/all_gather | solution.py:16
  36.3 14.2 %all_gather.17 = bf16[384,384]{0,1:T(8,128)(2,1)S(1)} all-gather(bf16[384,48]{0,1:T(8,128)(2,1)S(1)} %copy-done), channel_id=1, replica_groups=mesh['blk'=4,'grp'=8] {'grp'}, dimensions={1}, use_global_device_ids=true | all-gather | bytes 331776 | tf_op jit(solution)/shard_map/all_gather | solution.py:17
  50.6 0.2 copy.27
  50.8 0.9 gather_fusion.1
  51.7 0.1 copy.28
  52.0 0.6 pad_clamp_fusion
  52.6 1.4 gather_fusion
  54.1 0.6 gather_fusion.2
  54.7 290.2 %all-gather.3.cloned.1.call-done = bf16[384,3,32,512]{3,2,1,0:T(8,128)(2,1)} async-done(((bf16[96,3,32,512]{3,2,1,0:T(8,128)(2,1)}), bf16[384,3,32,512]{3,2,1,0:T(8,128)(2,1)}) %all-gather.3.cloned.1.call-update) | async-done | bytes 37748752 | tf_op jit(solution)/shard_map/all_gather | solution.py:29
  344.8 36.7 %bitcast_convert_fusion = bf16[12,160,32,512]{3,1,2,0:T(8,128)(2,1)} fusion(bf16[12,32,3,32,512]{4,3,2,1,0:T(8,128)(2,1)} %bitcast.86, bf16[12,3,160,32]{2,3,1,0:T(8,128)(2,1)S(1)} %bitcast.73, pred[12,3]{1,0:T(8,128)(4,1)S(1)} %compare_and_fusion), kind=kOutput, calls=%fused_computation.4 | convolution fusion | flops 6071439360 | bytes 101031968 | tf_op jit(solution)/shard_map/wlds,ladsq->lawq/dot_general | solution.py:38
  381.5 56.2 %copy.44 = bf16[48,8,160,512]{3,1,2,0:T(8,128)(2,1)} copy(bf16[48,8,160,512]{3,2,1,0:T(8,128)(2,1)} %bitcast.71) | data formatting | bytes 125829120
  437.7 80.5 %copy.29 = bf16[81920,384]{1,0:T(8,128)(2,1)} copy(bf16[81920,384]{0,1:T(8,128)(2,1)} %bitcast.70) | data formatting | bytes 125829120 | tf_op jit(solution)/shard_map/dot_general | solution.py:40
  518.2 31.3 %convolution_convert_fusion = bf16[96,160,512]{2,0,1:T(8,128)(2,1)} fusion(bf16[160,512,384]{2,1,0:T(8,128)(2,1)} %bitcast.69, bf16[384,96]{1,0:T(8,128)(2,1)S(1)} %gather_fusion, pred[384]{0:T(512)(128)(4,1)S(1)} %iota_compare_fusion.2), kind=kOutput, calls=%fused_computation.9 | convolution fusion | flops 6047698944 | bytes 78717312 | tf_op jit(solution)/shard_map/dot_general | solution.py:40
  549.5 4.3 fusion.23
  553.8 0.6 copy.31
  554.4 0.6 copy.32
  555.0 0.6 copy.33
  555.5 0.6 copy.34
  556.1 0.6 copy.35
  556.7 0.6 copy.36
  557.3 0.6 copy.37
  557.9 0.6 copy.38
  558.5 0.6 copy.39
  559.1 1.1 bitcast_dynamic-update-slice_fusion.8
  560.1 1.1 bitcast_dynamic-update-slice_fusion.7
  561.2 1.0 bitcast_dynamic-update-slice_fusion.6
  562.2 1.1 bitcast_dynamic-update-slice_fusion.5
  563.3 1.0 bitcast_dynamic-update-slice_fusion.4
  564.4 1.0 bitcast_dynamic-update-slice_fusion.3
  565.4 1.1 bitcast_dynamic-update-slice_fusion.2
  566.5 1.1 bitcast_dynamic-update-slice_fusion.1
  567.5 1.0 bitcast_dynamic-update-slice_fusion
  568.6 16.6 %gather_fusion.3 = bf16[32,1024,512]{2,1,0:T(8,128)(2,1)} fusion(bf16[9,1024,512]{2,1,0:T(8,128)(2,1)} %bitcast_dynamic-update-slice_fusion, s32[1024]{0:T(1024)} %pad_clamp_fusion), kind=kCustom, calls=%fused_computation.3 | custom fusion | bytes 67108992 | tf_op jit(solution)/shard_map/jit(_take)/gather | solution.py:57
  585.2 14.7 %fusion = f32[32,512,32]{1,2,0:T(8,128)S(1)} fusion(bf16[32,32,1024]{2,1,0:T(8,128)(2,1)} %all-gather.5.cloned.1.call-done, bf16[32,1024,512]{2,1,0:T(8,128)(2,1)} %gather_fusion.3, pred[32]{0:T(512)(128)(4,1)S(1)} %copy-done.4), kind=kOutput, calls=%fused_computation.5 | convolution fusion | flops 1090519040 | bytes 37748768 | tf_op jit(solution)/shard_map/tik,tkq->tiq/dot_general | solution.py:58
  599.9 1.2 copy.45
  601.1 0.8 fusion.18
  601.9 1.2 reshape.142
  603.1 28.1 %reduce-scatter.2.cloned.1.call-done = f32[128,512]{1,0:T(8,128)} async-done(((f32[512,512]{1,0:T(8,128)}), f32[128,512]{1,0:T(8,128)}) %reduce-scatter.2.cloned.1.call-update) | async-done | bytes 262160 | tf_op jit(solution)/shard_map/reduce_scatter | solution.py:66
  (31 shorter events, 0.4 us)
Async XLA Ops:
  6.5 1.6 copy-start.5
  6.5 2.9 copy-start.3
  6.5 15.9 %copy-start.1 = (bf16[96,48]{0,1:T(8,128)(2,1)S(1)}, bf16[96,48]{0,1:T(8,128)(2,1)}, u32[]{:S(2)}) copy-start(bf16[96,48]{0,1:T(8,128)(2,1)} %param.7) | copy-start | bytes 27652
  6.5 29.8 %copy-start = (bf16[384,48]{0,1:T(8,128)(2,1)S(1)}, bf16[384,48]{0,1:T(8,128)(2,1)}, u32[]{:S(2)}) copy-start(bf16[384,48]{0,1:T(8,128)(2,1)} %param.8) | copy-start | bytes 110596
  6.5 338.3 %all-gather.3.cloned.1.call-start = ((), (), s32[]{:S(2)}) async-start(), calls=%async_computation.1 | async-start | bytes 47185920 | tf_op jit(solution)/shard_map/all_gather | solution.py:29
  7.3 577.9 %all-gather.5.cloned.1.call-start = ((), (), s32[]{:S(2)}) async-start(), calls=%async_computation.2 | async-start | bytes 2359296 | tf_op jit(solution)/shard_map/all_gather | solution.py:51
  8.0 623.2 %reduce-scatter.2.cloned.1.call-start = ((), (), s32[]{:S(2)}) async-start(), calls=%async_computation.3 | async-start | bytes 1310720 | tf_op jit(solution)/shard_map/reduce_scatter | solution.py:66
  568.6 16.6 %copy-start.4 = (pred[32]{0:T(512)(128)(4,1)S(1)}, pred[32]{0:T(512)(128)(4,1)}, u32[]{:S(2)}) copy-start(pred[32]{0:T(512)(128)(4,1)} %get-tuple-element.5) | copy-start | bytes 100
  585.2 15.9 %copy-start.2 = (s32[32]{0:T(128)S(1)}, s32[32]{0:T(128)}, u32[]{:S(2)}) copy-start(s32[32]{0:T(128)} %compare_select_fusion.6) | copy-start | bytes 388
Sparse Core Ops, SparseCore 0:
  9.2 335.5 all-gather.2
  346.4 29.1 all-gather.4
  603.2 27.9 reduce-scatter.1
where the time goes:
time: 640 us; the launch traced here: 638 us
  waiting for transfers between devices  320 us (50%)
  local copies, waits for them, and re-layouts  179 us (28%)
  matrix products  83.5 us (13%)
  blocking collectives  38.8 us (6%)
  between operations  14 us (2%)
    all_gather x1, waiting for transfers between devices, local(): accumulate_piece = lax.all_gather(b3c, 'blk', axis=0, tiled=True)  290 us
    dot_general x1, local copies, waits for them, and re-layouts, local(): paired = jnp.dot(occ_cols, inner, preferred_element_type=jnp.float32)  80.5 us
    unnamed x25, local copies, waits for them, and re-layouts  66.7 us
    dot_general x1, matrix products, local(): jnp.einsum('wlds,ladsq->lawq', virt_sel, tensor, preferred_element_type=j...  36.7 us
    dot_general x1, matrix products, local(): paired = jnp.dot(occ_cols, inner, preferred_element_type=jnp.float32)  31.3 us
    reduce_scatter x1, waiting for transfers between devices, local(): return lax.psum_scatter(partial_chi, 'blk', scatter_dimension=0, tiled=True)  28.1 us
    gather x1, local copies, waits for them, and re-layouts, local(): chosen = jnp.take(pairs, pair, axis=0)  16.6 us
    dot_general x1, matrix products, local(): jnp.einsum('tik,tkq->tiq', tiles, chosen, preferred_element_type=jnp.floa...  14.7 us
  transfers between devices with their start and end apart: 3, of which 2 were waited for; matrix products, arithmetic and copies ran while one was open for 39% of the time, Pallas kernels for 0%

commit v1 on v0

--- a/solution.py
+++ b/solution.py
@@ -26,7 +26,13 @@
     occ_group = occ_all * mask_full
     rows = (group * KB * BS + jnp.arange(window, dtype=jnp.int32)) % basis_total
     virt_window = jnp.take(virt_all, rows, axis=0).reshape(window, block_total, BS)
-    accumulate_piece = lax.all_gather(b3c, "blk", axis=0, tiled=True)
+    size = lax.axis_size("blk")
+    moving, blocks = (b3c, [b3c])
+    for _ in range(size - 1):
+        moving = lax.ppermute(moving, "blk", [(i, (i + 1) % size) for i in range(size)])
+        blocks.insert(0, moving)
+    merged = jnp.concatenate(blocks, axis=0)
+    accumulate_piece = jnp.roll(merged, (lax.axis_index("blk") + 1) * b3c.shape[0], axis=0)
     count = accumulate_piece.shape[0]
     blocks_in = count // BS
     lam_index = jnp.arange(count, dtype=jnp.int32) % basis_total

time: 640 us -> 1010 us (1.58)
  waiting for transfers between devices: 320 us -> 592 us
  local copies, waits for them, and re-layouts: 179 us -> 277 us
    ppermute x0 -> x3, waiting for transfers between devices: none -> 564 us  [local(): lax.ppermute(moving, 'blk', [(i, (i + 1) % size) for i in range(size)])]
    all_gather x1 -> x0, waiting for transfers between devices: 290 us -> none  [local(): accumulate_piece = lax.all_gather(b3c, 'blk', axis=0, tiled=True)]
    unnamed x25 -> x30, local copies, waits for them, and re-layouts: 66.7 us -> 136 us
    dynamic_slice x0 -> x1, local copies, waits for them, and re-layouts: none -> 25.4 us  [local(): jnp.roll(merged, (lax.axis_index('blk') + 1) * b3c.shape[0], axis=0)]
  transfers between devices with their start and end apart: 3 -> 5, of which waited for: 2 -> 4; matrix products, arithmetic and copies ran while one was open for 39% -> 34% of each run, Pallas kernels for 0% -> 0%
where the time goes in v1:
time: 1010 us
  waiting for transfers between devices  592 us (59%)
  local copies, waits for them, and re-layouts  277 us (27%)
  matrix products  83.4 us (8%)
  blocking collectives  39.2 us (4%)
  between operations  14.2 us (1%)
    ppermute x3, waiting for transfers between devices, local(): lax.ppermute(moving, 'blk', [(i, (i + 1) % size) for i in range(size)])  564 us
    unnamed x30, local copies, waits for them, and re-layouts  136 us
    dot_general x1, local copies, waits for them, and re-layouts, local(): paired = jnp.dot(occ_cols, inner, preferred_element_type=jnp.float32)  73.1 us
    dot_general x1, matrix products, local(): jnp.einsum('wlds,ladsq->lawq', virt_sel, tensor, preferred_element_type=j...  36.5 us
    dot_general x1, matrix products, local(): paired = jnp.dot(occ_cols, inner, preferred_element_type=jnp.float32)  31.3 us
    reduce_scatter x1, waiting for transfers between devices, local(): return lax.psum_scatter(partial_chi, 'blk', scatter_dimension=0, tiled=True)  27.9 us
    dynamic_slice x1, local copies, waits for them, and re-layouts, local(): jnp.roll(merged, (lax.axis_index('blk') + 1) * b3c.shape[0], axis=0)  25.4 us
  transfers between devices with their start and end apart: 5, of which 4 were waited for; matrix products, arithmetic and copies ran while one was open for 34% of the time, Pallas kernels for 0%

profile of v1, /device:TPU:0, one launch (start us, length us, event | category | flops | bytes accessed | tf_op | source)
XLA Modules:
  0.0 1011.6 jit_solution(1579673558141053420)
XLA Ops:
  6.5 3.0 collective-permute-start
  9.5 204.1 %collective-permute-done = bf16[96,3,32,512]{3,2,1,0:T(8,128)(2,1)S(1)} collective-permute-done((bf16[96,3,32,512]{3,2,1,0:T(8,128)(2,1)}, bf16[96,3,32,512]{3,2,1,0:T(8,128)(2,1)S(1)}, u32[]{:S(2)}, u32[]{:S(2)}) %collective-permute-start) | collective-permute-done | bytes 9437216 | tf_op jit(solution)/shard_map/ppermute | solution.py:32
  213.6 3.7 copy-done
  217.3 0.8 collective-permute-start.1
  218.0 204.3 %collective-permute-done.1 = bf16[96,3,32,512]{3,2,1,0:T(8,128)(2,1)} collective-permute-done((bf16[96,3,32,512]{3,2,1,0:T(8,128)(2,1)S(1)}, bf16[96,3,32,512]{3,2,1,0:T(8,128)(2,1)}, u32[]{:S(2)}, u32[]{:S(2)}) %collective-permute-start.1) | collective-permute-done | bytes 9437216 | tf_op jit(solution)/shard_map/ppermute | solution.py:32
  422.5 14.6 %all_gather.14 = bf16[384,384]{0,1:T(8,128)(2,1)S(1)} all-gather(bf16[384,48]{0,1:T(8,128)(2,1)} %param.8), channel_id=1, replica_groups=mesh['blk'=4,'grp'=8] {'grp'}, dimensions={1}, use_global_device_ids=true | all-gather | bytes 331776 | tf_op jit(solution)/shard_map/all_gather | solution.py:17
  437.4 0.9 gather_fusion.1
  438.6 0.7 dynamic-slice_convert_fusion
  439.6 0.6 gather_fusion.2
  440.2 15.5 %all_gather.13 = bf16[96,384]{0,1:T(8,128)(2,1)S(1)} all-gather(bf16[96,48]{0,1:T(8,128)(2,1)} %param.7), channel_id=1, replica_groups=mesh['blk'=4,'grp'=8] {'grp'}, dimensions={1}, use_global_device_ids=true | all-gather | bytes 82944 | tf_op jit(solution)/shard_map/all_gather | solution.py:16
  455.7 1.9 gather_fusion
  457.6 1.2 dynamic-slice
  459.4 0.9 dynamic-update-slice
  460.3 9.0 all-reduce
  470.4 0.6 pad_clamp_fusion
  471.6 155.2 %collective-permute-done.2 = bf16[96,3,32,512]{3,2,1,0:T(8,128)(2,1)} collective-permute-done((bf16[96,3,32,512]{3,2,1,0:T(8,128)(2,1)}, bf16[96,3,32,512]{3,2,1,0:T(8,128)(2,1)}, u32[]{:S(2)}, u32[]{:S(2)}) %collective-permute-start.2) | collective-permute-done | bytes 9437216 | tf_op jit(solution)/shard_map/ppermute | solution.py:32
  626.8 9.3 constant_dynamic-update-slice_fusion.7
  636.1 9.3 constant_dynamic-update-slice_fusion.6
  645.3 9.3 constant_dynamic-update-slice_fusion.5
  654.7 9.3 constant_dynamic-update-slice_fusion.4
  663.9 9.2 constant_dynamic-update-slice_fusion.3
  673.1 9.2 constant_dynamic-update-slice_fusion.2
  682.3 9.2 constant_dynamic-update-slice_fusion.1
  691.5 9.1 constant_dynamic-update-slice_fusion
  700.6 25.4 %constant_dynamic-slice_fusion = bf16[384,3,32,512]{3,2,1,0:T(8,128)(2,1)} fusion(bf16[768,3,32,512]{3,2,1,0:T(8,128)(2,1)} %constant_dynamic-update-slice_fusion, s32[]{:T(128)S(6)} %select_n.147), kind=kLoop, calls=%fused_computation.70 | loop fusion | bytes 75497472 | tf_op jit(solution)/shard_map/jit(_roll_dynamic)/dynamic_slice | solution.py:35
  726.0 36.5 %bitcast_convert_fusion = bf16[12,32,512,160]{2,3,1,0:T(8,128)(2,1)} fusion(bf16[12,32,3,32,512]{4,3,2,1,0:T(8,128)(2,1)} %bitcast.72, bf16[12,3,160,32]{2,3,1,0:T(8,128)(2,1)S(1)} %bitcast.73, pred[12,3]{1,0:T(8,128)(4,1)S(1)} %compare_and_fusion), kind=kOutput, calls=%fused_computation.4 | convolution fusion | flops 6071439360 | bytes 101031968 | tf_op jit(solution)/shard_map/wlds,ladsq->lawq/dot_general | solution.py:44
  762.6 56.2 %copy.44 = bf16[48,8,160,512]{3,1,2,0:T(8,128)(2,1)} copy(bf16[48,8,160,512]{3,2,1,0:T(8,128)(2,1)} %bitcast.70) | data formatting | bytes 125829120
  818.8 73.1 %copy.29 = bf16[81920,384]{1,0:T(8,128)(2,1)} copy(bf16[81920,384]{0,1:T(8,128)(2,1)} %bitcast.71) | data formatting | bytes 125829120 | tf_op jit(solution)/shard_map/dot_general | solution.py:46
  891.9 31.3 %convolution_convert_fusion = bf16[96,160,512]{2,0,1:T(8,128)(2,1)} fusion(bf16[160,512,384]{2,1,0:T(8,128)(2,1)} %bitcast.69, bf16[384,96]{1,0:T(8,128)(2,1)S(1)} %copy-done.1, pred[384]{0:T(512)(128)(4,1)S(1)} %copy-done.3), kind=kOutput, calls=%fused_computation.9 | convolution fusion | flops 6047698944 | bytes 78717312 | tf_op jit(solution)/shard_map/dot_general | solution.py:46
  923.2 4.4 fusion.23
  927.5 0.6 copy.31
  928.7 0.6 copy.33
  929.9 0.6 copy.35
  932.8 1.1 bitcast_dynamic-update-slice_fusion.8
  933.9 1.1 bitcast_dynamic-update-slice_fusion.7
  935.0 1.0 bitcast_dynamic-update-slice_fusion.6
  936.0 1.1 bitcast_dynamic-update-slice_fusion.5
  937.1 1.0 bitcast_dynamic-update-slice_fusion.4
  938.2 1.0 bitcast_dynamic-update-slice_fusion.3
  939.2 1.1 bitcast_dynamic-update-slice_fusion.2
  940.3 1.1 bitcast_dynamic-update-slice_fusion.1
  941.3 1.0 bitcast_dynamic-update-slice_fusion
  942.4 16.6 %gather_fusion.3 = bf16[32,1024,512]{2,1,0:T(8,128)(2,1)} fusion(bf16[9,1024,512]{2,1,0:T(8,128)(2,1)} %bitcast_dynamic-update-slice_fusion, s32[1024]{0:T(1024)} %pad_clamp_fusion), kind=kCustom, calls=%fused_computation.3 | custom fusion | bytes 67108992 | tf_op jit(solution)/shard_map/jit(_take)/gather | solution.py:63
  959.0 14.7 %fusion = f32[32,512,32]{1,2,0:T(8,128)S(1)} fusion(bf16[32,32,1024]{2,1,0:T(8,128)(2,1)} %all-gather.2.cloned.1.call-done, bf16[32,1024,512]{2,1,0:T(8,128)(2,1)} %gather_fusion.3, pred[32]{0:T(512)(128)(4,1)S(1)} %copy-done.4), kind=kOutput, calls=%fused_computation.5 | convolution fusion | flops 1090519040 | bytes 37748768 | tf_op jit(solution)/shard_map/tik,tkq->tiq/dot_general | solution.py:64
  973.7 1.2 copy.45
  974.9 0.8 fusion.18
  975.8 1.2 reshape.142
  976.9 27.9 %reduce-scatter.2.cloned.1.call-done = f32[128,512]{1,0:T(8,128)} async-done(((f32[512,512]{1,0:T(8,128)}), f32[128,512]{1,0:T(8,128)}) %reduce-scatter.2.cloned.1.call-update) | async-done | bytes 262160 | tf_op jit(solution)/shard_map/reduce_scatter | solution.py:72
  (41 shorter events, 6.1 us)
Async XLA Ops:
  6.5 952.4 %all-gather.2.cloned.1.call-start = ((), (), s32[]{:S(2)}) async-start(), calls=%async_computation.1 | async-start | bytes 2359296 | tf_op jit(solution)/shard_map/all_gather | solution.py:57
  6.5 207.1 %collective-permute-start = (bf16[96,3,32,512]{3,2,1,0:T(8,128)(2,1)}, bf16[96,3,32,512]{3,2,1,0:T(8,128)(2,1)S(1)}, u32[]{:S(2)}, u32[]{:S(2)}) collective-permute-start(bf16[96,3,32,512]{3,2,1,0:T(8,128)(2,1)} %param.6), channel_id=1, source_target_pairs={{0,8},{8,16},{16,24},{24,0},{1,9},{9,17},{17,25},{25,1},{2,10},{10... | collective-permute-start | bytes 28311560 | tf_op jit(solution)/shard_map/ppermute | solution.py:32
  213.6 3.7 copy-start
  217.3 205.1 %collective-permute-start.1 = (bf16[96,3,32,512]{3,2,1,0:T(8,128)(2,1)S(1)}, bf16[96,3,32,512]{3,2,1,0:T(8,128)(2,1)}, u32[]{:S(2)}, u32[]{:S(2)}) collective-permute-start(bf16[96,3,32,512]{3,2,1,0:T(8,128)(2,1)S(1)} %collective-permute-done), channel_id=1, source_target_pairs={{0,8},{8,16},{16,24},{24,0},{1,9},{9,17},{17,25},{25,1},{2,10},{10... | collective-permute-start | bytes 28311560 | tf_op jit(solution)/shard_map/ppermute | solution.py:32
  422.4 204.4 %collective-permute-start.2 = (bf16[96,3,32,512]{3,2,1,0:T(8,128)(2,1)}, bf16[96,3,32,512]{3,2,1,0:T(8,128)(2,1)}, u32[]{:S(2)}, u32[]{:S(2)}) collective-permute-start(bf16[96,3,32,512]{3,2,1,0:T(8,128)(2,1)} %collective-permute-done.1), channel_id=1, source_target_pairs={{0,8},{8,16},{16,24},{24,0},{1,9},{9,17},{17,25},{25,1},{2,10},{10... | collective-permute-start | bytes 28311560 | tf_op jit(solution)/shard_map/ppermute | solution.py:32
  422.4 582.4 %reduce-scatter.2.cloned.1.call-start = ((), (), s32[]{:S(2)}) async-start(), calls=%async_computation.2 | async-start | bytes 1310720 | tf_op jit(solution)/shard_map/reduce_scatter | solution.py:72
  818.8 73.1 %copy-start.1 = (bf16[384,96]{1,0:T(8,128)(2,1)S(1)}, bf16[384,96]{1,0:T(8,128)(2,1)}, u32[]{:S(2)}) copy-start(bf16[384,96]{1,0:T(8,128)(2,1)} %gather_fusion) | copy-start | bytes 221188
  818.8 73.1 %copy-start.3 = (pred[384]{0:T(512)(128)(4,1)S(1)}, pred[384]{0:T(512)(128)(4,1)}, u32[]{:S(2)}) copy-start(pred[384]{0:T(512)(128)(4,1)} %iota_compare_fusion.2) | copy-start | bytes 1156
  942.4 16.6 %copy-start.4 = (pred[32]{0:T(512)(128)(4,1)S(1)}, pred[32]{0:T(512)(128)(4,1)}, u32[]{:S(2)}) copy-start(pred[32]{0:T(512)(128)(4,1)} %get-tuple-element.5) | copy-start | bytes 100
  959.0 15.9 %copy-start.2 = (s32[32]{0:T(128)S(1)}, s32[32]{0:T(128)}, u32[]{:S(2)}) copy-start(s32[32]{0:T(128)} %compare_select_fusion.6) | copy-start | bytes 388
Sparse Core Ops, SparseCore 0:
  422.5 32.3 all-gather.1
  977.1 27.6 reduce-scatter.1
